TPU v7x, 32 devices: a whole 2x2x4 slice. The times are simulated.
32 devices in a mesh: groups: 2 (over y), heads: 4 (over z), batch: 4 (over x, core).
Axes of the slice: x: 2, y: 2, z: 4, core: 2. Of those that a mesh axis runs over, the one named last changes fastest.
Arguments:
- queries: bfloat16 [128, 8192], P(('groups', 'batch'), 'heads'), parts along dimension 0, may hold values from -110 to 110
- new_kv: bfloat16 [16, 64, 256], P(('groups', 'heads'), 'batch'), parts along dimension 0, may hold values from -15 to 15
- kv_pool: bfloat16 [16, 192, 128, 256], P(('groups', 'heads'), 'batch'), parts along dimension 0, may hold values from -6 to 6
- page_counts: int32 [8, 16], P(('groups', 'batch')), parts along dimension 0, may hold values from 1 to 6, 48 in all within a row
- last_fill: int32 [8, 16], P(('groups', 'batch')), parts along dimension 0, may hold values from 1 to 128
- page_order: int32 [8, 48], P(('groups', 'batch')), parts along dimension 0, may hold values from 0 to 47, each once within a row
- hidden: bfloat16 [128, 8192], P(('groups', 'batch')), parts along dimension 0, may hold values from -0.59765625 to 0.59765625
- out_weight: bfloat16 [8192, 8192], P('heads'), may hold values from -0.5 to 0.5
- norm_gain: bfloat16 [8192], replicated, may hold values from 0.099609375 to 1.8984375
- sectioned: bfloat16 [8, 4, 8, 128, 256], P(('groups', 'heads'), 'batch'), parts along dimension 0, may hold values from -6 to 6
- routes: int32 [8, 4, 8, 1], P(('groups', 'heads'), 'batch'), parts along dimension 0, may hold values from 0 to 7; in each aligned block of 8 rows (0 to 7, 8 to 15, ..., all dimensions but the last counted through in order) at most 2 rows name the same one
Outputs:
- residual_out: bfloat16 [128, 8192], P(('groups', 'batch')), parts along dimension 0
- normed: bfloat16 [128, 8192], P(('groups', 'batch')), parts along dimension 0
- arrival: bfloat16 [16, 4, 4, 2, 128, 256], P(('groups', 'heads'), 'batch'), parts along dimension 0
There are 2 independent parts, one for each index of `groups`. A program takes and returns all parts, laid end to end along the dimension named above; an argument that names none is the same for every part. Nothing has to cross between parts.
Inputs may be any that keep to these rules, and one draw needn't show every extreme that they name: `routes`: every key-value head is named by at most 2 sectioned pages of one device. `page_counts`: the page counts of one batch owner sum to 48.
All inputs are finite; a program needn't handle non-finite values.
Results may differ from a plain program's by a relative error of at most 0.0066.
Values may be sent and summed in bfloat16 or wider, within the bound.
A program may use at most 128 MiB of HBM per device.

v0:
```python
import jax
import jax.numpy as jnp
from jax import lax
from jax.sharding import PartitionSpec as P

KV_HEADS = 8
PER_HEAD_CAP = 2
norm_epsilon = 1e-06


def attend(queries, new_kv, kv_pool, counts, fill, order):
    slot_count, pool_pages, page_size, lane_width = kv_pool.shape
    head_dim = lane_width // 2
    requests = queries.shape[0]
    score_scale = 1.0 / head_dim**0.5
    position = jnp.arange(pool_pages, dtype=jnp.int32)
    position_in_order = jnp.sum(
        jnp.where(order[None, :] == position[:, None], position[None, :], 0), axis=1
    )
    count_ends = jnp.cumsum(counts)
    starts = count_ends - counts
    owner_index = jnp.sum(
        (count_ends[None, :] <= position_in_order[:, None]).astype(jnp.int32), axis=1
    )
    member = owner_index[:, None] == jnp.arange(requests, dtype=jnp.int32)[None, :]
    member_float = member.astype(jnp.float32)
    within = position_in_order - jnp.sum(jnp.where(member, starts[None, :], 0), axis=1)
    context = (counts - 1) * page_size + fill
    context_limit = jnp.sum(jnp.where(member, context[None, :], 0), axis=1)
    live_tokens = (
        within[:, None] * page_size + jnp.arange(page_size, dtype=jnp.int32)[None, :]
        < context_limit[:, None]
    )
    page_queries = jnp.einsum(
        "pr,rlgd->lpgd", member.astype(jnp.bfloat16), queries, preferred_element_type=jnp.float32
    ).astype(jnp.bfloat16)
    scores = (
        jnp.einsum(
            "lpgd,lptd->lpgt",
            page_queries,
            kv_pool[..., :head_dim],
            preferred_element_type=jnp.float32,
        )
        * score_scale
    )
    scores = jnp.where(live_tokens[None, :, None, :], scores, -1e30)
    page_top = jnp.max(scores, axis=3)
    fresh_score = (
        jnp.einsum(
            "rlgd,lrd->lrg", queries, new_kv[..., :head_dim], preferred_element_type=jnp.float32
        )
        * score_scale
    )
    masked_top = jnp.where(member.T[None, :, :, None], page_top[:, None, :, :], -1e30)
    request_top = jnp.maximum(fresh_score, jnp.max(masked_top, axis=2))
    page_ref = jnp.einsum("pr,lrg->lpg", member_float, request_top, precision=lax.Precision.HIGHEST)
    weight = jnp.where(live_tokens[None, :, None, :], jnp.exp(scores - page_ref[..., None]), 0.0)
    page_den = jnp.sum(weight, axis=3)
    page_num = jnp.einsum(
        "lpgt,lptd->lpgd",
        weight.astype(jnp.bfloat16),
        kv_pool[..., head_dim:],
        preferred_element_type=jnp.float32,
    )
    fresh_weight = jnp.exp(fresh_score - request_top)
    fresh_rounded = lax.optimization_barrier(fresh_weight.astype(jnp.bfloat16)).astype(jnp.float32)
    denominator = (
        jnp.einsum("pr,lpg->lrg", member_float, page_den, precision=lax.Precision.HIGHEST)
        + fresh_weight
    )
    numerator = jnp.einsum("pr,lpgd->lrgd", member_float, page_num, precision=lax.Precision.HIGHEST)
    numerator = numerator + fresh_rounded[..., None] * new_kv[:, :, None, head_dim:].astype(
        jnp.float32
    )
    attended = numerator / denominator[..., None]
    attended = jnp.transpose(attended, (1, 0, 2, 3)).astype(jnp.bfloat16)
    return attended.reshape(requests, -1)


def landing_table(destination, head_total, most_pages):
    sectioned_count = destination.shape[0]
    order_ids = jnp.arange(sectioned_count, dtype=jnp.int32)
    same_head = destination[:, None] == destination[None, :]
    earlier = order_ids[:, None] > order_ids[None, :]
    page_rank = jnp.sum((same_head & earlier).astype(jnp.int32), axis=1)
    matches = (
        destination[None, None, :] == jnp.arange(head_total, dtype=jnp.int32)[:, None, None]
    ) & (page_rank[None, None, :] == jnp.arange(most_pages, dtype=jnp.int32)[None, :, None])
    source_index = jnp.sum(jnp.where(matches, order_ids[None, None, :], 0), axis=2)
    source_valid = jnp.any(matches, axis=2)
    return (source_index, source_valid)


def per_device(
    queries,
    new_kv,
    kv_pool,
    page_counts,
    last_fill,
    page_order,
    hidden,
    out_weight,
    norm_gain,
    sectioned,
    routes,
):
    head_count = lax.axis_size("heads")
    slots_dev = new_kv.shape[0]
    head_dim = kv_pool.shape[3] // 2
    requests = hidden.shape[0]
    group_size = queries.shape[1] // (slots_dev * head_dim)
    page_data = sectioned[0, 0]
    source_index, source_valid = landing_table(routes[0, 0, :, 0], KV_HEADS, PER_HEAD_CAP)
    cache_total = head_count * slots_dev
    target = (
        (
            jnp.arange(head_count, dtype=jnp.int32)[None, :] * slots_dev
            + jnp.arange(slots_dev, dtype=jnp.int32)[:, None]
        )
        * KV_HEADS
        // cache_total
    )
    picked = source_index[target]
    present = source_valid[target]
    outgoing = page_data[picked]
    outgoing = jnp.where(present[..., None, None], outgoing, jnp.zeros_like(outgoing))
    landed = lax.all_to_all(outgoing, "heads", split_axis=1, concat_axis=1, tiled=True)
    arrival = landed[:, None]
    query_block = queries.reshape(requests, slots_dev, group_size, head_dim)
    attn = attend(query_block, new_kv, kv_pool, page_counts[0], last_fill[0], page_order[0])
    partial_terms = jnp.dot(attn, out_weight, preferred_element_type=jnp.float32)
    summed = lax.psum(partial_terms, "heads")
    mixed = hidden.astype(jnp.float32) + summed
    mean_square = jnp.mean(mixed * mixed, axis=1, keepdims=True)
    normed = (mixed * lax.rsqrt(mean_square + norm_epsilon) * norm_gain.astype(jnp.float32)).astype(
        jnp.bfloat16
    )
    residual_out = mixed.astype(jnp.bfloat16)
    return (residual_out, normed, arrival)


def solution(mesh):
    return jax.shard_map(
        per_device,
        mesh=mesh,
        in_specs=(
            P(("groups", "batch"), "heads"),
            P(("groups", "heads"), "batch", None),
            P(("groups", "heads"), "batch", None, None),
            P(("groups", "batch"), None),
            P(("groups", "batch"), None),
            P(("groups", "batch"), None),
            P(("groups", "batch"), None),
            P("heads", None),
            P(),
            P(("groups", "heads"), "batch", None, None, None),
            P(("groups", "heads"), "batch", None, None),
        ),
        out_specs=(
            P(("groups", "batch"), None),
            P(("groups", "batch"), None),
            P(("groups", "heads"), "batch", None, None, None, None),
        ),
        check_vma=False,
    )
```

profile of v0, /device:TPU:0, one launch (start us, length us, event | category | flops | bytes accessed | tf_op | source)
XLA Modules:
  0.0 96.6 jit_solution(1213633889777169506)
XLA Ops:
  7.2 0.0 copy-start
  7.2 0.0 all-reduce.2.cloned.1.call-start
  7.2 0.8 select_reduce_fusion.1
  8.0 0.7 copy.69
  8.8 0.1 reduce
  8.9 0.1 convert_reduce_fusion
  9.0 0.7 add_bitcast_fusion
  9.7 0.1 select_reduce_fusion.3
  9.8 0.7 convert_bitcast_fusion
  10.5 0.8 copy.93
  11.4 0.3 fusion.10
  11.6 0.1 fusion.27
  11.8 0.1 copy.90
  11.9 0.1 add_compare_fusion
  12.0 3.7 %fusion.48 = (f32[2,48,8]{2,1,0:T(8,128)S(1)}, f32[2,48,8,128]{3,2,1,0:T(8,128)S(1)}) fusion(bf16[2,48,128,256]{3,2,1,0:T(8,128)(2,1)} %param.13, bf16[2,48,8,128]{3,1,2,0:T(8,128)(2,1)S(1)} %fusion.10, pred[48,128]{1,0:T(8,128)(4,1)S(1)} %add_compare_fusion), kind=kOutput, calls=%fused_computation.86 | convolution fusion | flops 25459968 | bytes 3744768 | tf_op jit(solution)/shard_map/lpgd,lptd->lpgt/dot_general | solution.py:38
  15.7 0.1 copy.72
  15.7 0.1 select_reduce_fusion
  15.9 0.1 copy.73
  15.9 0.1 convolution_bitcast_fusion.1
  16.1 0.1 copy.74
  16.2 0.3 fusion.15
  16.5 2.9 %fusion = f32[2,48,8,128]{3,2,1,0:T(8,128)S(1)} fusion(bf16[2,48,128,256]{3,2,1,0:T(8,128)(2,1)} %param.13, f32[2,48,8,128]{3,2,1,0:T(8,128)S(1)} %get-tuple-element.24, f32[2,48,8]{2,1,0:T(8,128)S(1)} %copy.74, pred[48,128]{1,0:T(8,128)(4,1)S(1)} %add_compare_fusion), kind=kOutput, calls=%fused_computation.3 | convolution fusion | flops 25460736 | bytes 3941376 | tf_op jit(solution)/shard_map/lpgt,lptd->lpgd/dot_general | solution.py:59
  19.3 0.1 copy.76
  19.4 0.1 fusion.13
  19.6 0.3 fusion.12
  19.9 0.0 copy-start.3
  19.9 13.7 %fusion.23 = f32[16,8192]{1,0:T(8,128)} fusion(bf16[2048,8192]{1,0:T(8,128)(2,1)} %param.18, bf16[2,8,16,128]{3,2,1,0:T(8,128)(2,1)S(1)} %bitcast.73), kind=kOutput, calls=%fused_computation.31 | convolution fusion | flops 536870912 | bytes 34144256 | tf_op jit(solution)/shard_map/dot_general | solution.py:131
  33.6 0.0 all-reduce.2.cloned.1.call-update
  33.6 0.2 convert_reduce_fusion.1
  33.8 0.1 and_reduce_fusion
  34.0 0.2 fusion.30
  34.2 0.1 reshape.257
  34.2 0.1 copy.79
  34.3 0.1 copy.82
  34.4 0.6 gather_fusion.1
  35.0 0.6 gather_fusion
  35.6 0.1 copy.92
  35.7 0.1 copy.84
  35.8 0.1 reshape.273
  35.9 0.6 gather_fusion.2
  36.5 0.1 broadcast_select_fusion
  36.6 1.1 %copy.85 = bf16[2,4,2,128,256]{4,3,2,0,1:T(8,128)(2,1)} copy(bf16[2,4,2,128,256]{4,3,2,1,0:T(8,128)(2,1)S(1)} %broadcast_select_fusion) | data formatting | bytes 2097152 | tf_op jit(solution)/shard_map/jit(_where)/select_n | solution.py:126
  37.7 6.3 %all-to-all-start = ((bf16[2,4,2,128,256]{4,3,2,0,1:T(8,128)(2,1)}), bf16[2,4,2,128,256]{4,3,2,0,1:T(8,128)(2,1)S(1)}, u32[]{:S(2)}, u32[]{:S(2)}) async-start(bf16[2,4,2,128,256]{4,3,2,0,1:T(8,128)(2,1)} %copy.85), calls=%async_computation | async-start | bytes 2097152 | tf_op jit(solution)/shard_map/all_to_all | solution.py:127
  44.1 41.5 %all-reduce.2.cloned.1.call-done = f32[16,8192]{1,0:T(8,128)} async-done(((f32[16,8192]{1,0:T(8,128)}), f32[16,8192]{1,0:T(8,128)}) %all-reduce.2.cloned.1.call-update) | async-done | bytes 524304 | tf_op jit(solution)/shard_map/psum | solution.py:132
  85.6 1.2 %multiply_reduce_fusion = f32[16]{0:T(128)S(1)} fusion(f32[16,8192]{1,0:T(8,128)} %all-reduce.2.cloned.1.call-done, bf16[16,8192]{1,0:T(8,128)(2,1)S(1)} %copy-done.1), kind=kLoop, calls=%fused_computation.19 | loop fusion | flops 524272 | bytes 786496 | tf_op jit(solution)/shard_map/reduce_sum | solution.py:134
  86.8 1.9 %multiply_convert_fusion = (bf16[16,8192]{1,0:T(8,128)(2,1)}, bf16[16,8192]{1,0:T(8,128)(2,1)}) fusion(f32[8192]{0:T(1024)S(1)} %convert_element_type.46, f32[16]{0:T(128)S(1)} %add_rsqrt_fusion, f32[16,8192]{1,0:T(8,128)} %all-reduce.2.cloned.1.call-done, bf16[16,8192]{1,0:T(8,128)(2,1)S(1)} %copy-done.1), kind=kLoop, calls=%fused_computation.18 | loop fusion | flops 786432 | bytes 1343552 | tf_op jit(solution)/shard_map/convert_element_type | solution.py:135
  88.7 0.0 all-to-all-done
  88.7 1.0 %copy.86 = bf16[2,1,4,2,128,256]{5,4,3,2,1,0:T(8,128)(2,1)} copy(bf16[2,1,4,2,128,256]{5,4,3,0,2,1:T(8,128)(2,1)S(1)} %bitcast.71) | data formatting | bytes 2097152
  (21 shorter events, 0.2 us)
Async XLA Ops:
  7.2 28.7 %copy-start = (bf16[1,1,8,128,256]{4,3,2,1,0:T(8,128)(2,1)S(1)}, bf16[1,1,8,128,256]{4,3,2,1,0:T(8,128)(2,1)}, u32[]{:S(2)}) copy-start(bf16[1,1,8,128,256]{4,3,2,1,0:T(8,128)(2,1)} %param.20) | copy-start | bytes 1572868
  7.2 78.4 %all-reduce.2.cloned.1.call-start = ((), (), s32[]{:S(2)}) async-start(), calls=%async_computation.1 | async-start | bytes 1048576 | tf_op jit(solution)/shard_map/psum | solution.py:132
  19.9 13.7 %copy-start.3 = (s32[1,1,8,1]{2,3,1,0:T(1,128)S(1)}, s32[1,1,8,1]{2,3,1,0:T(1,128)}, u32[]{:S(2)}) copy-start(s32[1,1,8,1]{2,3,1,0:T(1,128)} %param.21) | copy-start | bytes 100
  33.6 10.5 %copy-start.2 = (bf16[8192]{0:T(1024)(128)(2,1)S(1)}, bf16[8192]{0:T(1024)(128)(2,1)}, u32[]{:S(2)}) copy-start(bf16[8192]{0:T(1024)(128)(2,1)} %param.19) | copy-start | bytes 49156
  33.6 52.0 %copy-start.1 = (bf16[16,8192]{1,0:T(8,128)(2,1)S(1)}, bf16[16,8192]{1,0:T(8,128)(2,1)}, u32[]{:S(2)}) copy-start(bf16[16,8192]{1,0:T(8,128)(2,1)} %param.17) | copy-start | bytes 786436
  37.7 51.0 %all-to-all-start = ((bf16[2,4,2,128,256]{4,3,2,0,1:T(8,128)(2,1)}), bf16[2,4,2,128,256]{4,3,2,0,1:T(8,128)(2,1)S(1)}, u32[]{:S(2)}, u32[]{:S(2)}) async-start(bf16[2,4,2,128,256]{4,3,2,0,1:T(8,128)(2,1)} %copy.85), calls=%async_computation | async-start | bytes 2097152 | tf_op jit(solution)/shard_map/all_to_all | solution.py:127
Sparse Core Ops, SparseCore 0:
  33.7 51.7 all-reduce.1
where the time goes:
time: 97.1 us; the launch traced here: 96.6 us
  waiting for transfers between devices  41.5 us (43%)
  matrix products  21.2 us (22%)
  between operations  14.2 us (15%)
  other arithmetic  6.9 us (7%)
  local copies, waits for them, and re-layouts  6.39 us (7%)
  starting transfers between devices  6.38 us (7%)
    psum x1, waiting for transfers between devices, per_device(): summed = lax.psum(partial_terms, 'heads')  41.5 us
    dot_general x1, matrix products, per_device(): jnp.dot(attn, out_weight, preferred_element_type=jnp.float32)  13.7 us
    all_to_all x1, starting transfers between devices, per_device(): lax.all_to_all(outgoing, 'heads', split_axis=1, concat_axis=1, tiled=True)  6.35 us
    dot_general x1, matrix products, attend(): jnp.einsum('lpgd,lptd->lpgt', page_queries, kv_pool[..., :head_dim], pref...  3.69 us
    dot_general x1, matrix products, attend(): jnp.einsum('lpgt,lptd->lpgd', weight.astype(jnp.bfloat16), kv_pool[..., h...  2.86 us
  transfers between devices with their start and end apart: 2, of which 1 were waited for; matrix products, arithmetic and copies ran while one was open for 7% of the time, Pallas kernels for 0%

commit v1 on v0

--- a/solution.py
+++ b/solution.py
@@ -129,7 +129,7 @@
     query_block = queries.reshape(requests, slots_dev, group_size, head_dim)
     attn = attend(query_block, new_kv, kv_pool, page_counts[0], last_fill[0], page_order[0])
     partial_terms = jnp.dot(attn, out_weight, preferred_element_type=jnp.float32)
-    summed = lax.psum(partial_terms, "heads")
+    summed = jnp.sum(lax.all_gather(partial_terms, "heads"), axis=0)
     mixed = hidden.astype(jnp.float32) + summed
     mean_square = jnp.mean(mixed * mixed, axis=1, keepdims=True)
     normed = (mixed * lax.rsqrt(mean_square + norm_epsilon) * norm_gain.astype(jnp.float32)).astype(

time: 97.1 us -> 114 us (1.17)
  waiting for transfers between devices: 41.5 us -> 58.8 us
    all_to_all x1, waiting for transfers between devices: 0.01 us -> 52.5 us  [per_device(): lax.all_to_all(outgoing, 'heads', split_axis=1, concat_axis=1, tiled=True)]
    psum x1 -> x0, waiting for transfers between devices: 41.5 us -> none  [per_device(): summed = lax.psum(partial_terms, 'heads')]
    all_gather x0 -> x1, waiting for transfers between devices: none -> 6.31 us  [per_device(): summed = jnp.sum(lax.all_gather(partial_terms, 'heads'), axis=0)]
    reduce_sum x0 -> x1, other arithmetic: none -> 1.76 us  [per_device(): summed = jnp.sum(lax.all_gather(partial_terms, 'heads'), axis=0)]
  transfers between devices with their start and end apart: 2 -> 2, of which waited for: 1 -> 2; matrix products, arithmetic and copies ran while one was open for 7% -> 4% of each run, Pallas kernels for 0% -> 0%
where the time goes in v1:
time: 114 us
  waiting for transfers between devices  58.8 us (52%)
  matrix products  21.2 us (19%)
  between operations  14.2 us (12%)
  other arithmetic  6.55 us (6%)
  local copies, waits for them, and re-layouts  6.45 us (6%)
  starting transfers between devices  6.38 us (6%)
    all_to_all x1, waiting for transfers between devices, per_device(): lax.all_to_all(outgoing, 'heads', split_axis=1, concat_axis=1, tiled=True)  52.5 us
    dot_general x1, matrix products, per_device(): jnp.dot(attn, out_weight, preferred_element_type=jnp.float32)  13.7 us
    all_to_all x1, starting transfers between devices, per_device(): lax.all_to_all(outgoing, 'heads', split_axis=1, concat_axis=1, tiled=True)  6.35 us
    all_gather x1, waiting for transfers between devices, per_device(): summed = jnp.sum(lax.all_gather(partial_terms, 'heads'), axis=0)  6.31 us
    dot_general x1, matrix products, attend(): jnp.einsum('lpgd,lptd->lpgt', page_queries, kv_pool[..., :head_dim], pref...  3.69 us
    dot_general x1, matrix products, attend(): jnp.einsum('lpgt,lptd->lpgd', weight.astype(jnp.bfloat16), kv_pool[..., h...  2.86 us
  transfers between devices with their start and end apart: 2, of which 2 were waited for; matrix products, arithmetic and copies ran while one was open for 4% of the time, Pallas kernels for 0%

profile of v1, /device:TPU:0, one launch (start us, length us, event | category | flops | bytes accessed | tf_op | source)
XLA Modules:
  0.0 113.6 jit_solution(872474187472810435)
XLA Ops:
  7.2 0.0 copy-start
  7.2 0.0 all-gather.3.cloned.1.call-start
  7.2 0.8 copy.69
  8.0 0.1 reduce
  8.2 0.8 select_reduce_fusion.1
  8.9 0.1 convert_reduce_fusion
  9.0 0.7 add_bitcast_fusion
  9.7 0.1 select_reduce_fusion.3
  9.8 0.9 copy.93
  10.7 0.3 fusion.10
  10.9 0.1 add_compare_fusion
  11.0 3.7 %fusion.48 = (f32[2,48,8]{2,1,0:T(8,128)S(1)}, f32[2,48,8,128]{3,2,1,0:T(8,128)S(1)}) fusion(bf16[2,48,128,256]{3,2,1,0:T(8,128)(2,1)} %param.13, bf16[2,48,8,128]{3,1,2,0:T(8,128)(2,1)S(1)} %fusion.10, pred[48,128]{1,0:T(8,128)(4,1)S(1)} %add_compare_fusion), kind=kOutput, calls=%fused_computation.86 | convolution fusion | flops 25459968 | bytes 3744768 | tf_op jit(solution)/shard_map/lpgd,lptd->lpgt/dot_general | solution.py:38
  14.7 0.1 copy.72
  14.8 0.1 select_reduce_fusion
  14.9 0.1 copy.73
  15.0 0.7 convert_bitcast_fusion
  15.7 0.1 fusion.27
  15.8 0.1 copy.90
  15.9 0.1 convolution_bitcast_fusion.1
  16.0 0.1 copy.74
  16.2 0.3 fusion.15
  16.5 2.9 %fusion = f32[2,48,8,128]{3,2,1,0:T(8,128)S(1)} fusion(bf16[2,48,128,256]{3,2,1,0:T(8,128)(2,1)} %param.13, f32[2,48,8,128]{3,2,1,0:T(8,128)S(1)} %get-tuple-element.24, f32[2,48,8]{2,1,0:T(8,128)S(1)} %copy.74, pred[48,128]{1,0:T(8,128)(4,1)S(1)} %add_compare_fusion), kind=kOutput, calls=%fused_computation.3 | convolution fusion | flops 25460736 | bytes 3941376 | tf_op jit(solution)/shard_map/lpgt,lptd->lpgd/dot_general | solution.py:59
  19.4 0.1 copy.76
  19.4 0.1 fusion.13
  19.6 0.3 fusion.12
  19.9 13.7 %fusion.23 = f32[16,8192]{1,0:T(8,128)} fusion(bf16[2048,8192]{1,0:T(8,128)(2,1)} %param.18, bf16[2,8,16,128]{3,2,1,0:T(8,128)(2,1)S(1)} %bitcast.75), kind=kOutput, calls=%fused_computation.31 | convolution fusion | flops 536870912 | bytes 34144256 | tf_op jit(solution)/shard_map/dot_general | solution.py:131
  33.6 0.0 all-gather.3.cloned.1.call-update
  33.6 0.2 convert_reduce_fusion.1
  33.8 0.1 fusion.30
  34.0 0.1 copy.82
  34.1 0.1 reshape.257
  34.2 0.6 gather_fusion.1
  34.7 0.1 copy.92
  34.8 0.1 copy.84
  34.9 0.1 reshape.273
  35.0 0.1 and_reduce_fusion
  35.2 0.1 copy.79
  35.3 0.6 gather_fusion
  35.9 0.6 gather_fusion.2
  36.5 0.1 broadcast_select_fusion
  36.6 1.1 copy.85
  37.7 6.3 %all-to-all-start = ((bf16[2,4,2,128,256]{4,3,2,0,1:T(8,128)(2,1)}), bf16[2,4,2,128,256]{4,3,2,0,1:T(8,128)(2,1)S(1)}, u32[]{:S(2)}, u32[]{:S(2)}) async-start(bf16[2,4,2,128,256]{4,3,2,0,1:T(8,128)(2,1)} %copy.85), calls=%async_computation | async-start | bytes 2097152 | tf_op jit(solution)/shard_map/all_to_all | solution.py:127
  44.1 52.5 %all-to-all-done = bf16[2,4,2,128,256]{4,3,2,0,1:T(8,128)(2,1)S(1)} async-done(((bf16[2,4,2,128,256]{4,3,2,0,1:T(8,128)(2,1)}), bf16[2,4,2,128,256]{4,3,2,0,1:T(8,128)(2,1)S(1)}, u32[]{:S(2)}, u32[]{:S(2)}) %all-to-all-start) | async-done | bytes 1048608 | tf_op jit(solution)/shard_map/all_to_all | solution.py:127
  96.6 1.0 copy.86
  97.6 6.3 %all-gather.3.cloned.1.call-done = f32[64,8192]{1,0:T(8,128)} async-done(((f32[16,8192]{1,0:T(8,128)}), f32[64,8192]{1,0:T(8,128)}) %all-gather.3.cloned.1.call-update) | async-done | bytes 2097168 | tf_op jit(solution)/shard_map/all_gather | solution.py:132
  103.9 1.8 %reduce_sum.86 = f32[16,8192]{1,0:T(8,128)S(1)} reduce(f32[4,16,8192]{2,1,0:T(8,128)} %bitcast.74, f32[]{:T(128)} %constant.13.clone.1), dimensions={0}, to_apply=%region_8.9 | reduce | flops 393216 | bytes 2621444 | tf_op jit(solution)/shard_map/reduce_sum | solution.py:132
  105.7 0.2 multiply_reduce_fusion
  105.9 0.9 multiply_convert_fusion
  (22 shorter events, 0.2 us)
Async XLA Ops:
  7.2 28.7 %copy-start = (bf16[1,1,8,128,256]{4,3,2,1,0:T(8,128)(2,1)S(1)}, bf16[1,1,8,128,256]{4,3,2,1,0:T(8,128)(2,1)}, u32[]{:S(2)}) copy-start(bf16[1,1,8,128,256]{4,3,2,1,0:T(8,128)(2,1)} %param.20) | copy-start | bytes 1572868
  7.2 96.7 %all-gather.3.cloned.1.call-start = ((), (), s32[]{:S(2)}) async-start(), calls=%async_computation.1 | async-start | bytes 2621440 | tf_op jit(solution)/shard_map/all_gather | solution.py:132
  19.9 13.7 %copy-start.3 = (s32[1,1,8,1]{2,3,1,0:T(1,128)S(1)}, s32[1,1,8,1]{2,3,1,0:T(1,128)}, u32[]{:S(2)}) copy-start(s32[1,1,8,1]{2,3,1,0:T(1,128)} %param.21) | copy-start | bytes 100
  33.6 10.5 %copy-start.2 = (bf16[8192]{0:T(1024)(128)(2,1)S(1)}, bf16[8192]{0:T(1024)(128)(2,1)}, u32[]{:S(2)}) copy-start(bf16[8192]{0:T(1024)(128)(2,1)} %param.19) | copy-start | bytes 49156
  35.9 69.8 %copy-start.1 = (bf16[16,8192]{1,0:T(8,128)(2,1)S(1)}, bf16[16,8192]{1,0:T(8,128)(2,1)}, u32[]{:S(2)}) copy-start(bf16[16,8192]{1,0:T(8,128)(2,1)} %param.17) | copy-start | bytes 786436
  37.7 58.9 %all-to-all-start = ((bf16[2,4,2,128,256]{4,3,2,0,1:T(8,128)(2,1)}), bf16[2,4,2,128,256]{4,3,2,0,1:T(8,128)(2,1)S(1)}, u32[]{:S(2)}, u32[]{:S(2)}) async-start(bf16[2,4,2,128,256]{4,3,2,0,1:T(8,128)(2,1)} %copy.85), calls=%async_computation | async-start | bytes 2097152 | tf_op jit(solution)/shard_map/all_to_all | solution.py:127
Sparse Core Ops, SparseCore 0:
  33.7 70.1 all-gather.2
